TPU v7x, 512 devices: a 4x2x32 block of a 4x8x32 slice. The times are simulated.
512 devices in a mesh: grp: 2 (over y), sp: 128 (over x, z), ch: 2 (over core).
Axes of the slice: x: 4, y: 2, z: 32, core: 2. Of those that a mesh axis runs over, the one named last changes fastest.
The devices are a block of a 4x8x32 slice.
Arguments:
- latents: bfloat16 [262144, 1024], P(('grp', 'sp')), parts along dimension 0, may hold values from -6 to 6
- spectrum: bfloat16 [16, 64, 128, 1024], P(None, None, 'sp', 'ch'), may hold values from -4 to 4
- w_value: bfloat16 [1024, 1024], P('sp', 'ch'), may hold values from -0.1875 to 0.1875
- w_gate: bfloat16 [1024, 1024], P('sp', 'ch'), may hold values from -0.1875 to 0.1875
- w_out: bfloat16 [1024, 1024], P('sp'), may hold values from -0.1875 to 0.1875
- embed_table: bfloat16 [1024, 32768], P(('sp', 'ch')), may hold values from -12 to 12
- prompt_ids: int32 [512], P('grp'), parts along dimension 0, may hold values from 0 to 32767
- noise_step: int32 [2], P('grp'), parts along dimension 0, may hold values from 0 to 999
Outputs:
- denoised: bfloat16 [262144, 1024], P(('grp', 'sp', 'ch')), parts along dimension 0
There are 2 independent parts, one for each index of `grp`. A program takes and returns all parts, laid end to end along the dimension named above; an argument that names none is the same for every part. Nothing has to cross between parts.
All inputs are finite; a program needn't handle non-finite values.
Results may differ from a plain program's by a relative error of at most 0.013.
Values may be sent and summed in bfloat16 or wider, within the bound.
A program may use at most 64 MiB of HBM per device.

v0:
```python
import math
import jax
import jax.numpy as jnp
from jax import lax
from jax.sharding import Mesh
from jax.sharding import PartitionSpec as P

TT = 16
HH = 64
WW = 128
C = 1024
SP = ("sp_0", "sp_1")
SP_CH = ("sp_0", "sp_1", "ch")
GRP_SP = ("grp", "sp_0", "sp_1")
GRP_SP_CH = ("grp", "sp_0", "sp_1", "ch")
F32 = jnp.float32
BF16 = jnp.bfloat16


def cas_table(length):
    position = jnp.arange(length, dtype=jnp.int32)
    product = position[:, None] * position[None, :] % length
    phase_angle = product.astype(jnp.float32) * (2.0 * math.pi / length)
    return ((jnp.cos(phase_angle) + jnp.sin(phase_angle)) / math.sqrt(length)).astype(jnp.bfloat16)


def step_embedding(noise_step, channel, channels):
    half_count = channels // 2
    lower_half = channel < half_count
    position = jnp.where(lower_half, channel, channel - half_count).astype(jnp.float32)
    frequency = jnp.exp(-math.log(10000.0) * position / half_count)
    phase_angle = noise_step[0].astype(jnp.float32) * frequency
    return jnp.where(lower_half, jnp.sin(phase_angle), jnp.cos(phase_angle))


def dot(a, b):
    return jnp.dot(a, b, preferred_element_type=F32)


def local_pool(embed_table, prompt_ids):
    vocab = embed_table.shape[1]
    low = 256
    high_hot = (prompt_ids[:, None] // low == jnp.arange(vocab // low)[None, :]).astype(BF16)
    low_hot = (prompt_ids[:, None] % low == jnp.arange(low)[None, :]).astype(BF16)
    counts = jnp.einsum("ph,pl->hl", high_hot, low_hot, preferred_element_type=F32)
    total = jnp.sum(embed_table.astype(F32) * counts.reshape(1, vocab), axis=1)
    return total / prompt_ids.shape[0]


def local(latents, spectrum, w_value, w_gate, w_out, embed_table, prompt_ids, noise_step):
    row_count = latents.shape[0]
    part = w_value.shape[1]
    lines = row_count // WW
    core = lax.axis_index("ch")
    offset = core * part
    pool4 = local_pool(embed_table, prompt_ids)
    pool8 = lax.all_gather(pool4, "ch", axis=0, tiled=True)
    high = lax.reduce_precision(pool8, 8, 7)
    low = pool8 - high
    pool_cols = jnp.pad(jnp.stack([high, low], axis=1), ((0, 0), (0, 126))).astype(BF16)
    packed = jnp.concatenate([w_value, w_gate, w_out, pool_cols], axis=1)
    column = lax.all_gather(packed, "sp_1", axis=0, tiled=True)
    weights = lax.all_gather(column, "sp_0", axis=0, tiled=True)
    cas_width = cas_table(WW)
    space = jnp.einsum("st,ah->sath", cas_table(TT).astype(F32), cas_table(HH).astype(F32))
    space = space.reshape(TT * HH, TT * HH).astype(BF16)
    mine = lax.dynamic_slice_in_dim(latents, offset, part, 1).reshape(lines, WW, part)
    spread = jnp.einsum("kw,lwc->klc", cas_width, mine, preferred_element_type=F32).astype(BF16)
    arrived = lax.all_to_all(spread, SP, split_axis=0, concat_axis=0, tiled=True)
    arrived = arrived.reshape(TT * HH, part)
    both = lax.all_gather(arrived, "ch", axis=1, tiled=True)
    width_spec = dot(both, weights[:, :part]).astype(BF16)
    full_spec = dot(space, width_spec).astype(BF16)
    gains = spectrum.reshape(TT * HH, part)
    filtered = (full_spec.astype(F32) * gains.astype(F32)).astype(BF16)
    height_back = dot(space, filtered).astype(BF16)
    returned = lax.all_to_all(
        height_back.reshape(-1, lines, part), SP, split_axis=0, concat_axis=0, tiled=True
    )
    gate_rows = dot(latents, weights[:, part : 2 * part])
    pooled_all = weights[:, 2 * part + C].astype(F32) + weights[:, 2 * part + C + 1].astype(F32)
    pooled = lax.dynamic_slice_in_dim(pooled_all, offset, part)
    channel = offset + jnp.arange(part, dtype=jnp.int32)
    modulation = 1.0 + pooled + step_embedding(noise_step, channel, C)
    gain = jax.nn.silu(gate_rows) * modulation[None, :]
    mix_rows = jnp.einsum("wk,klc->lwc", cas_width, returned, preferred_element_type=F32)
    mixed = (mix_rows.reshape(row_count, part) * gain).astype(BF16)
    half = row_count // lax.axis_size("ch")
    moved = lax.all_to_all(mixed, "ch", split_axis=0, concat_axis=1, tiled=True)
    summed = dot(moved, weights[:, 2 * part : 2 * part + C])
    residual = lax.dynamic_slice_in_dim(latents, core * half, half, 0)
    return (residual.astype(F32) + summed).astype(BF16)


def solution(mesh):
    torus = Mesh(
        mesh.devices.reshape(mesh.shape["grp"], 4, 32, mesh.shape["ch"]),
        ("grp", "sp_0", "sp_1", "ch"),
    )
    in_specs = (
        P(GRP_SP, None),
        P(None, None, SP, "ch"),
        P(SP, "ch"),
        P(SP, "ch"),
        P(SP, None),
        P(SP_CH, None),
        P("grp"),
        P("grp"),
    )
    out_specs = P(GRP_SP_CH, None)
    return jax.shard_map(local, mesh=torus, in_specs=in_specs, out_specs=out_specs, check_vma=False)
```

profile of v0, /device:TPU:33, one launch (start us, length us, event | category | flops | bytes accessed | tf_op | source)
XLA Modules:
  0.0 464.0 jit_solution(6335007486320289089)
XLA Ops:
  6.5 0.0 all-gather.6.cloned.1.call-start
  6.6 0.7 and_select_fusion.1
  7.2 0.3 convolution_bitcast_fusion
  7.5 0.1 copy.24
  7.6 1.3 dynamic-slice.1
  9.5 1.3 multiply_reduce_fusion
  10.9 0.1 multiply_dynamic-update-slice_fusion
  11.0 43.6 %all-reduce.1 = f32[8]{0:T(128)S(1)} all-reduce(f32[8]{0:T(128)S(1)} %multiply_dynamic-update-slice_fusion), channel_id=1, replica_groups=mesh['grp'=2,'sp_0'=4,'sp_1'=32,'ch'=2] {'ch'}, use_global_device_ids=true, to_apply=%add.1 | all-reduce | flops 8 | bytes 64
  54.6 0.1 copy.22
  54.7 1.4 fusion.28
  56.0 0.1 all-gather.6.cloned.1.call-update
  56.1 1.3 constant_dynamic-slice_fusion
  57.4 0.7 convolution_convert_fusion.3
  58.1 1.5 copy.17
  59.6 12.9 %all-to-all-start = ((bf16[128,8,512]{2,1,0:T(8,128)(2,1)}), bf16[128,8,512]{2,1,0:T(8,128)(2,1)S(1)}, u32[]{:S(2)}, u32[]{:S(2)}) async-start(bf16[128,8,512]{2,1,0:T(8,128)(2,1)} %copy.17), calls=%async_computation | async-start | bytes 2097152 | tf_op jit(solution)/shard_map/all_to_all | solution.py:69
  72.5 0.1 all-gather.8.cloned.1.call-start
  72.6 118.9 %all-gather.6.cloned.1.call-done = bf16[256,2176]{1,0:T(8,128)(2,1)} async-done(((bf16[8,2176]{1,0:T(8,128)(2,1)}), bf16[256,2176]{1,0:T(8,128)(2,1)}) %all-gather.6.cloned.1.call-update) | async-done | bytes 1114128 | tf_op jit(solution)/shard_map/all_gather | solution.py:62
  191.5 0.1 all-gather.8.cloned.1.call-update
  191.6 0.1 all-gather.4.cloned.1.call-start
  191.6 0.0 all-to-all-done
  191.7 0.0 copy-start
  191.7 1.0 copy-done
  192.6 0.1 all-gather.4.cloned.1.call-update
  192.7 0.1 fusion.51
  192.8 0.1 fusion.44
  192.9 3.0 fusion
  195.9 0.0 copy-start.2
  195.9 5.6 %convert_element_type.98 = bf16[1024,1024]{1,0:T(8,128)(2,1)S(1)} reshape(bf16[16,64,16,64]{3,2,1,0:T(8,128)(2,1)} %fusion) | data formatting | bytes 4194304 | tf_op jit(solution)/shard_map/convert_element_type | solution.py:66
  201.4 62.7 %all-gather.8.cloned.1.call-done = bf16[1024,2176]{1,0:T(8,128)(2,1)} async-done(((bf16[256,2176]{1,0:T(8,128)(2,1)}), bf16[1024,2176]{1,0:T(8,128)(2,1)}) %all-gather.8.cloned.1.call-update) | async-done | bytes 4456464 | tf_op jit(solution)/shard_map/all_gather | solution.py:63
  264.2 35.1 %all-gather.4.cloned.1.call-done = bf16[1024,1024]{1,0:T(8,128)(2,1)} async-done(((bf16[1024,512]{1,0:T(8,128)(2,1)}), bf16[1024,1024]{1,0:T(8,128)(2,1)}) %all-gather.4.cloned.1.call-update) | async-done | bytes 2097168 | tf_op jit(solution)/shard_map/all_gather | solution.py:71
  299.3 0.0 copy-done.2
  299.3 5.2 %fusion.3 = bf16[1024,512]{1,0:T(8,128)(2,1)} fusion(bf16[1024,512]{1,0:T(8,128)(2,1)S(1)} %bitcast.64, bf16[1024,1024]{1,0:T(8,128)(2,1)S(1)} %convert_element_type.98, bf16[1024,1024]{1,0:T(8,128)(2,1)} %all-gather.4.cloned.1.call-done, bf16[1024,2176]{1,0:T(8,128)(2,1)} %all-gather.8.cloned.1.call-done), kind=kOutput, calls=%fused_computation.5 | convolution fusion | flops 2150629376 | bytes 7340032 | tf_op jit(solution)/shard_map/dot_general | solution.py:37
  304.5 3.5 fusion.12
  307.9 28.1 %all-to-all-start.1 = ((bf16[128,8,512]{2,1,0:T(8,128)(2,1)}), bf16[128,8,512]{2,1,0:T(8,128)(2,1)S(1)}, u32[]{:S(2)}, u32[]{:S(2)}) async-start(bf16[128,8,512]{2,1,0:T(8,128)(2,1)} %fusion.12), calls=%async_computation.1 | async-start | bytes 2097152 | tf_op jit(solution)/shard_map/all_to_all | solution.py:77
  336.7 1.2 fusion.70
  337.9 0.2 add_reduce_fusion
  338.1 0.1 fusion.52
  338.1 101.6 %all-to-all-done.1 = bf16[128,8,512]{2,1,0:T(8,128)(2,1)S(1)} async-done(((bf16[128,8,512]{2,1,0:T(8,128)(2,1)}), bf16[128,8,512]{2,1,0:T(8,128)(2,1)S(1)}, u32[]{:S(2)}, u32[]{:S(2)}) %all-to-all-start.1) | async-done | bytes 1048608 | tf_op jit(solution)/shard_map/all_to_all | solution.py:77
  439.7 1.1 fusion.15
  440.8 1.9 copy.20
  442.6 4.2 fusion.9
  446.8 0.0 copy-start.1
  446.9 0.1 copy.28
  446.9 6.7 %all_to_all.29 = bf16[2,512,512]{1,2,0:T(8,128)(2,1)S(1)} all-to-all(bf16[2,512,512]{1,2,0:T(8,128)(2,1)S(1)} %bitcast.60), channel_id=1, replica_groups=mesh['grp'=2,'sp_0'=4,'sp_1'=32,'ch'=2] {'ch'}, dimensions={0} | all-to-all | bytes 2097152 | tf_op jit(solution)/shard_map/all_to_all | solution.py:89
  453.6 0.0 copy-done.1
  453.6 3.8 add_convert_fusion
  (3 shorter events, 0.0 us)
Async XLA Ops:
  6.5 185.0 %all-gather.6.cloned.1.call-start = ((), (), s32[]{:S(2)}) async-start(), calls=%async_computation.4 | async-start | bytes 1148928 | tf_op jit(solution)/shard_map/all_gather | solution.py:62
  59.6 132.0 %all-to-all-start = ((bf16[128,8,512]{2,1,0:T(8,128)(2,1)}), bf16[128,8,512]{2,1,0:T(8,128)(2,1)S(1)}, u32[]{:S(2)}, u32[]{:S(2)}) async-start(bf16[128,8,512]{2,1,0:T(8,128)(2,1)} %copy.17), calls=%async_computation | async-start | bytes 2097152 | tf_op jit(solution)/shard_map/all_to_all | solution.py:69
  72.5 191.7 %all-gather.8.cloned.1.call-start = ((), (), s32[]{:S(2)}) async-start(), calls=%async_computation.5 | async-start | bytes 5570560 | tf_op jit(solution)/shard_map/all_gather | solution.py:63
  191.6 107.7 %all-gather.4.cloned.1.call-start = ((), (), s32[]{:S(2)}) async-start(), calls=%async_computation.3 | async-start | bytes 3145728 | tf_op jit(solution)/shard_map/all_gather | solution.py:71
  191.7 1.0 copy-start
  195.9 103.4 %copy-start.2 = (bf16[16,64,1,512]{3,1,2,0:T(8,128)(2,1)S(1)}, bf16[16,64,1,512]{3,1,2,0:T(8,128)(2,1)}, u32[]{:S(2)}) copy-start(bf16[16,64,1,512]{3,1,2,0:T(8,128)(2,1)} %param.9) | copy-start | bytes 3145732
  307.9 131.8 %all-to-all-start.1 = ((bf16[128,8,512]{2,1,0:T(8,128)(2,1)}), bf16[128,8,512]{2,1,0:T(8,128)(2,1)S(1)}, u32[]{:S(2)}, u32[]{:S(2)}) async-start(bf16[128,8,512]{2,1,0:T(8,128)(2,1)} %fusion.12), calls=%async_computation.1 | async-start | bytes 2097152 | tf_op jit(solution)/shard_map/all_to_all | solution.py:77
  446.8 6.8 %copy-start.1 = (bf16[1024,1024]{1,0:T(8,128)(2,1)S(1)}, bf16[1024,1024]{1,0:T(8,128)(2,1)}, u32[]{:S(2)}) copy-start(bf16[1024,1024]{1,0:T(8,128)(2,1)} %param.8) | copy-start | bytes 6291460
Sparse Core Ops, SparseCore 0:
  56.2 135.2 all-gather.5
  193.6 70.4 all-gather.7
  266.3 32.9 all-gather.3
where the time goes:
time: 465 us; the launch traced here: 464 us
  waiting for transfers between devices  319 us (69%)
  blocking collectives  50.3 us (11%)
  starting transfers between devices  41.1 us (9%)
  matrix products  18.7 us (4%)
  between operations  14.6 us (3%)
  local copies, waits for them, and re-layouts  13.9 us (3%)
  other arithmetic  6.88 us (1%)
    all_gather x1, waiting for transfers between devices, local(): column = lax.all_gather(packed, 'sp_1', axis=0, tiled=True)  119 us
    all_to_all x1, waiting for transfers between devices, local(): lax.all_to_all(height_back.reshape(-1, lines, part), SP, split_axis=0, co...  102 us
    all_gather x1, waiting for transfers between devices, local(): weights = lax.all_gather(column, 'sp_0', axis=0, tiled=True)  62.7 us
    unnamed x1, blocking collectives  43.6 us
    all_gather x1, waiting for transfers between devices, local(): both = lax.all_gather(arrived, 'ch', axis=1, tiled=True)  35.1 us
    all_to_all x1, starting transfers between devices, local(): lax.all_to_all(height_back.reshape(-1, lines, part), SP, split_axis=0, co...  28.1 us
    dot_general x4, matrix products, dot(): return jnp.dot(a, b, preferred_element_type=F32)  16.7 us
    all_to_all x1, starting transfers between devices, local(): lax.all_to_all(spread, SP, split_axis=0, concat_axis=0, tiled=True)  12.9 us
  transfers between devices with their start and end apart: 5, of which 4 were waited for; matrix products, arithmetic and copies ran while one was open for 3% of the time, Pallas kernels for 0%

commit v1 on v0

--- a/solution.py
+++ b/solution.py
@@ -60,7 +60,8 @@
     pool_cols = jnp.pad(jnp.stack([high, low], axis=1), ((0, 0), (0, 126))).astype(BF16)
     packed = jnp.concatenate([w_value, w_gate, w_out, pool_cols], axis=1)
     column = lax.all_gather(packed, "sp_1", axis=0, tiled=True)
-    weights = lax.all_gather(column, "sp_0", axis=0, tiled=True)
+    repeated = jnp.stack([column] * lax.axis_size("sp_0"))
+    weights = jnp.concatenate(lax.all_to_all(repeated, "sp_0", 0, 0), axis=0)
     cas_width = cas_table(WW)
     space = jnp.einsum("st,ah->sath", cas_table(TT).astype(F32), cas_table(HH).astype(F32))
     space = space.reshape(TT * HH, TT * HH).astype(BF16)

time: 465 us -> 426 us (0.916)
  waiting for transfers between devices: 319 us -> 256 us
  starting transfers between devices: 41.1 us -> 84.6 us
  blocking collectives: 50.3 us -> 21 us
  local copies, waits for them, and re-layouts: 13.9 us -> 23.5 us
    all_gather x1 -> x0, waiting for transfers between devices: 62.7 us -> none  [local(): weights = lax.all_gather(column, 'sp_0', axis=0, tiled=True)]
    all_to_all x1, starting transfers between devices: 12.9 us -> 53.7 us  [local(): lax.all_to_all(spread, SP, split_axis=0, concat_axis=0, tiled=True)]
    unnamed x1, blocking collectives: 43.6 us -> 3.02 us
    all_gather x1, waiting for transfers between devices: 35.1 us -> 0.01 us  [local(): both = lax.all_gather(arrived, 'ch', axis=1, tiled=True)]
    all_to_all x0 -> x1, waiting for transfers between devices: none -> 27.5 us  [local(): weights = jnp.concatenate(lax.all_to_all(repeated, 'sp_0', 0, 0), axis=0)]
    all_gather x1, waiting for transfers between devices: 119 us -> 137 us  [local(): column = lax.all_gather(packed, 'sp_1', axis=0, tiled=True)]
    all_to_all x1, blocking collectives: 6.7 us -> 18 us  [local(): moved = lax.all_to_all(mixed, 'ch', split_axis=0, concat_axis=1, tiled=True)]
    all_to_all x1, waiting for transfers between devices: 102 us -> 91.3 us  [local(): lax.all_to_all(height_back.reshape(-1, lines, part), SP, split_axis=0, co...]
  transfers between devices with their start and end apart: 5 -> 5, of which waited for: 4 -> 3; matrix products, arithmetic and copies ran while one was open for 3% -> 5% of each run, Pallas kernels for 0% -> 0%
where the time goes in v1:
time: 426 us; the launch traced here: 425 us
  waiting for transfers between devices  256 us (60%)
  starting transfers between devices  84.6 us (20%)
  local copies, waits for them, and re-layouts  23.5 us (6%)
  blocking collectives  21 us (5%)
  matrix products  18.7 us (4%)
  between operations  16.4 us (4%)
  other arithmetic  4.55 us (1%)
    all_gather x1, waiting for transfers between devices, local(): column = lax.all_gather(packed, 'sp_1', axis=0, tiled=True)  137 us
    all_to_all x1, waiting for transfers between devices, local(): lax.all_to_all(height_back.reshape(-1, lines, part), SP, split_axis=0, co...  91.3 us
    all_to_all x1, starting transfers between devices, local(): lax.all_to_all(spread, SP, split_axis=0, concat_axis=0, tiled=True)  53.7 us
    all_to_all x1, waiting for transfers between devices, local(): weights = jnp.concatenate(lax.all_to_all(repeated, 'sp_0', 0, 0), axis=0)  27.5 us
    all_to_all x1, starting transfers between devices, local(): lax.all_to_all(height_back.reshape(-1, lines, part), SP, split_axis=0, co...  25.6 us
    all_to_all x1, blocking collectives, local(): moved = lax.all_to_all(mixed, 'ch', split_axis=0, concat_axis=1, tiled=True)  18 us
    dot_general x4, matrix products, dot(): return jnp.dot(a, b, preferred_element_type=F32)  16.7 us
  transfers between devices with their start and end apart: 5, of which 3 were waited for; matrix products, arithmetic and copies ran while one was open for 5% of the time, Pallas kernels for 0%

profile of v1, /device:TPU:33, one launch (start us, length us, event | category | flops | bytes accessed | tf_op | source)
XLA Modules:
  0.0 425.2 jit_solution(15691643045250507557)
XLA Ops:
  7.4 1.3 constant_dynamic-slice_fusion
  8.7 0.7 convolution_convert_fusion.3
  9.4 0.0 copy-start.6
  9.4 0.0 copy-start.2
  9.4 0.0 copy-start.3
  9.4 0.0 copy-start.4
  9.4 0.0 copy-start.5
  9.4 1.5 copy.24
  11.0 53.7 %all-to-all-start = ((bf16[128,8,512]{2,1,0:T(8,128)(2,1)}), bf16[128,8,512]{2,1,0:T(8,128)(2,1)S(1)}, u32[]{:S(2)}, u32[]{:S(2)}) async-start(bf16[128,8,512]{2,1,0:T(8,128)(2,1)} %copy.24), calls=%async_computation | async-start | bytes 2097152 | tf_op jit(solution)/shard_map/all_to_all | solution.py:70
  64.7 0.1 all-gather.5.cloned.1.call-start
  64.8 0.3 convolution_bitcast_fusion
  65.1 0.1 copy.33
  65.2 1.3 dynamic-slice.1
  67.1 0.4 multiply_reduce_fusion
  67.5 0.1 multiply_dynamic-update-slice_fusion
  67.6 3.0 all-reduce.1
  70.7 0.1 copy.31
  70.8 0.6 fusion.28
  71.4 0.1 all-gather.5.cloned.1.call-update
  71.4 137.2 %all-gather.5.cloned.1.call-done = bf16[256,2176]{1,0:T(8,128)(2,1)} async-done(((bf16[8,2176]{1,0:T(8,128)(2,1)}), bf16[256,2176]{1,0:T(8,128)(2,1)}) %all-gather.5.cloned.1.call-update) | async-done | bytes 1114128 | tf_op jit(solution)/shard_map/all_gather | solution.py:62
  208.7 1.6 copy.26
  210.3 0.0 all-to-all-done
  210.3 0.0 copy-start
  210.3 2.4 stack.22
  212.7 5.0 %all-to-all-start.1 = ((bf16[4,256,2176]{1,2,0:T(8,128)(2,1)}), bf16[4,256,2176]{1,2,0:T(8,128)(2,1)}, u32[]{:S(2)}, u32[]{:S(2)}) async-start(bf16[4,256,2176]{1,2,0:T(8,128)(2,1)} %stack.22), calls=%async_computation.1 | async-start | bytes 8912896 | tf_op jit(solution)/shard_map/all_to_all | solution.py:64
  217.8 0.2 all-gather.3.cloned.1.call-start
  218.0 0.4 all-gather.3.cloned.1.call-update
  218.4 0.1 fusion.51
  218.5 0.1 fusion.44
  218.6 3.0 fusion
  221.6 5.5 %convert_element_type.98 = bf16[1024,1024]{1,0:T(8,128)(2,1)S(1)} reshape(bf16[16,64,16,64]{3,2,1,0:T(8,128)(2,1)} %fusion) | data formatting | bytes 4194304 | tf_op jit(solution)/shard_map/convert_element_type | solution.py:67
  227.1 0.0 copy-start.7
  227.1 27.5 %all-to-all-done.1 = bf16[4,256,2176]{1,2,0:T(8,128)(2,1)} async-done(((bf16[4,256,2176]{1,2,0:T(8,128)(2,1)}), bf16[4,256,2176]{1,2,0:T(8,128)(2,1)}, u32[]{:S(2)}, u32[]{:S(2)}) %all-to-all-start.1) | async-done | bytes 4456480 | tf_op jit(solution)/shard_map/all_to_all | solution.py:64
  254.6 6.5 %copy.27 = bf16[4,256,2176]{2,1,0:T(8,128)(2,1)} copy(bf16[4,256,2176]{1,2,0:T(8,128)(2,1)} %all-to-all-done.1) | data formatting | bytes 8912896 | tf_op jit(solution)/shard_map/all_to_all | solution.py:64
  261.1 5.2 %fusion.3 = bf16[1024,512]{1,0:T(8,128)(2,1)} fusion(bf16[1024,512]{1,0:T(8,128)(2,1)S(1)} %bitcast.69, bf16[1024,1024]{1,0:T(8,128)(2,1)S(1)} %convert_element_type.98, bf16[1024,1024]{1,0:T(8,128)(2,1)} %all-gather.3.cloned.1.call-done, bf16[1024,2176]{1,0:T(8,128)(2,1)} %bitcast.59), kind=kOutput, calls=%fused_computation.5 | convolution fusion | flops 2150629376 | bytes 7340032 | tf_op jit(solution)/shard_map/dot_general | solution.py:37
  266.3 3.5 fusion.12
  269.7 25.6 %all-to-all-start.2 = ((bf16[128,8,512]{2,1,0:T(8,128)(2,1)}), bf16[128,8,512]{2,1,0:T(8,128)(2,1)S(1)}, u32[]{:S(2)}, u32[]{:S(2)}) async-start(bf16[128,8,512]{2,1,0:T(8,128)(2,1)} %fusion.12), calls=%async_computation.2 | async-start | bytes 2097152 | tf_op jit(solution)/shard_map/all_to_all | solution.py:78
  295.9 1.2 fusion.70
  297.1 0.2 add_reduce_fusion
  297.3 0.1 fusion.52
  297.4 91.3 %all-to-all-done.2 = bf16[128,8,512]{2,1,0:T(8,128)(2,1)S(1)} async-done(((bf16[128,8,512]{2,1,0:T(8,128)(2,1)}), bf16[128,8,512]{2,1,0:T(8,128)(2,1)S(1)}, u32[]{:S(2)}, u32[]{:S(2)}) %all-to-all-start.2) | async-done | bytes 1048608 | tf_op jit(solution)/shard_map/all_to_all | solution.py:78
  388.7 1.1 fusion.15
  389.8 1.9 copy.29
  391.6 4.2 fusion.9
  395.9 0.0 copy-start.1
  395.9 0.1 copy.37
  395.9 18.0 %all_to_all.34 = bf16[2,512,512]{1,2,0:T(8,128)(2,1)S(1)} all-to-all(bf16[2,512,512]{1,2,0:T(8,128)(2,1)S(1)} %bitcast.65), channel_id=1, replica_groups=mesh['grp'=2,'sp_0'=4,'sp_1'=32,'ch'=2] {'ch'}, dimensions={0} | all-to-all | bytes 2097152 | tf_op jit(solution)/shard_map/all_to_all | solution.py:90
  413.9 3.8 add_convert_fusion
  (13 shorter events, 0.1 us)
Async XLA Ops:
  9.4 55.4 %copy-start.6 = (s32[256]{0:T(256)S(1)}, s32[256]{0:T(256)}, u32[]{:S(2)}) copy-start(s32[256]{0:T(256)} %param.14) | copy-start | bytes 3076
  9.4 57.7 %copy-start.2 = (bf16[4,32768]{1,0:T(4,128)(2,1)S(1)}, bf16[4,32768]{1,0:T(4,128)(2,1)}, u32[]{:S(2)}) copy-start(bf16[4,32768]{1,0:T(4,128)(2,1)} %param.13) | copy-start | bytes 786436
  9.4 61.4 %copy-start.3 = (bf16[8,1024]{1,0:T(8,128)(2,1)S(1)}, bf16[8,1024]{1,0:T(8,128)(2,1)}, u32[]{:S(2)}) copy-start(bf16[8,1024]{1,0:T(8,128)(2,1)} %param.12) | copy-start | bytes 49156
  9.4 61.4 %copy-start.4 = (bf16[8,512]{1,0:T(8,128)(2,1)S(1)}, bf16[8,512]{1,0:T(8,128)(2,1)}, u32[]{:S(2)}) copy-start(bf16[8,512]{1,0:T(8,128)(2,1)} %param.11) | copy-start | bytes 24580
  9.4 61.4 %copy-start.5 = (bf16[8,512]{1,0:T(8,128)(2,1)S(1)}, bf16[8,512]{1,0:T(8,128)(2,1)}, u32[]{:S(2)}) copy-start(bf16[8,512]{1,0:T(8,128)(2,1)} %param.10) | copy-start | bytes 24580
  11.0 199.3 %all-to-all-start = ((bf16[128,8,512]{2,1,0:T(8,128)(2,1)}), bf16[128,8,512]{2,1,0:T(8,128)(2,1)S(1)}, u32[]{:S(2)}, u32[]{:S(2)}) async-start(bf16[128,8,512]{2,1,0:T(8,128)(2,1)} %copy.24), calls=%async_computation | async-start | bytes 2097152 | tf_op jit(solution)/shard_map/all_to_all | solution.py:70
  64.7 144.0 %all-gather.5.cloned.1.call-start = ((), (), s32[]{:S(2)}) async-start(), calls=%async_computation.5 | async-start | bytes 1148928 | tf_op jit(solution)/shard_map/all_gather | solution.py:62
  210.3 2.4 copy-start
  212.7 41.9 %all-to-all-start.1 = ((bf16[4,256,2176]{1,2,0:T(8,128)(2,1)}), bf16[4,256,2176]{1,2,0:T(8,128)(2,1)}, u32[]{:S(2)}, u32[]{:S(2)}) async-start(bf16[4,256,2176]{1,2,0:T(8,128)(2,1)} %stack.22), calls=%async_computation.1 | async-start | bytes 8912896 | tf_op jit(solution)/shard_map/all_to_all | solution.py:64
  217.8 43.3 %all-gather.3.cloned.1.call-start = ((), (), s32[]{:S(2)}) async-start(), calls=%async_computation.4 | async-start | bytes 3145728 | tf_op jit(solution)/shard_map/all_gather | solution.py:72
  227.1 34.0 %copy-start.7 = (bf16[16,64,1,512]{3,1,2,0:T(8,128)(2,1)S(1)}, bf16[16,64,1,512]{3,1,2,0:T(8,128)(2,1)}, u32[]{:S(2)}) copy-start(bf16[16,64,1,512]{3,1,2,0:T(8,128)(2,1)} %param.9) | copy-start | bytes 3145732
  269.7 119.0 %all-to-all-start.2 = ((bf16[128,8,512]{2,1,0:T(8,128)(2,1)}), bf16[128,8,512]{2,1,0:T(8,128)(2,1)S(1)}, u32[]{:S(2)}, u32[]{:S(2)}) async-start(bf16[128,8,512]{2,1,0:T(8,128)(2,1)} %fusion.12), calls=%async_computation.2 | async-start | bytes 2097152 | tf_op jit(solution)/shard_map/all_to_all | solution.py:78
  395.9 18.0 %copy-start.1 = (bf16[1024,1024]{1,0:T(8,128)(2,1)S(1)}, bf16[1024,1024]{1,0:T(8,128)(2,1)}, u32[]{:S(2)}) copy-start(bf16[1024,1024]{1,0:T(8,128)(2,1)} %param.8) | copy-start | bytes 6291460
Sparse Core Ops, SparseCore 0:
  71.6 137.0 all-gather.4
Sparse Core Ops, SparseCore 1:
  220.4 38.1 all-gather.2
